TPU v7x, 128 devices: a whole 4x4x4 slice. The times are simulated.
128 devices in a mesh: dp: 16 (over y, x_lo, core), shard: 8 (over z, x_hi).
Axes of the slice: x: 4 (x_hi: 2, x_lo: 2; x = x_hi * 2 + x_lo), y: 4, z: 4, core: 2. Of those that a mesh axis runs over, the one named last changes fastest.
Arguments:
- gradients: bfloat16 [16, 88, 512, 512], P('dp', 'shard'), may hold values from -60 to 60
- owners: int32 [8, 11], P('shard'), may hold values from 0 to 15, as said below
- block_param: int32 [88], replicated, may hold values from 0 to 6, never falling along the last dimension, each value on 1 to 25 neighbouring positions
- left_stat: float32 [32, 8, 512, 512], P('dp', 'shard'), may hold values from -4 to 8, as said below
- right_stat: float32 [32, 8, 512, 512], P('dp', 'shard'), may hold values from -4 to 8, as said below
- moment: float32 [32, 8, 512, 512], P('dp', 'shard'), may hold values from 0.5 to 50
- left_root: bfloat16 [32, 8, 512, 512], P('dp', 'shard'), may hold values from -1 to 3.5, as said below
- right_root: bfloat16 [32, 8, 512, 512], P('dp', 'shard'), may hold values from -1 to 3.5, as said below
Outputs:
- new_left: float32 [32, 8, 512, 512], P('dp', 'shard')
- new_right: float32 [32, 8, 512, 512], P('dp', 'shard')
- new_moment: float32 [32, 8, 512, 512], P('dp', 'shard')
- update: bfloat16 [88, 512, 512], P('shard')
Inputs may be any that keep to these rules, and one draw needn't show every extreme that they name: `owners`: in each row, no value occurs more than 2 times, and some value occurs exactly 2 times. `left_stat`: each slot's matrix is symmetric. `right_stat`: each slot's matrix is symmetric. `left_root`: each slot's matrix is symmetric. `right_root`: each slot's matrix is symmetric.
All inputs are finite; a program needn't handle non-finite values.
Results may differ from a plain program's by a relative error of at most 0.0058.
Values may be sent and summed in bfloat16 or wider, within the bound.
A program may use at most 192 MiB of HBM per device.

v0:
```python
import jax
import jax.numpy as jnp
from jax import lax
from jax.sharding import Mesh
from jax.sharding import PartitionSpec as P

NPARAM = 7
DP = ("dp_0", "dp_1", "dp_2")
SHARD = ("shard_0", "shard_1")
DP_SHARD = ("dp_0", "dp_1", "dp_2", "shard_0", "shard_1")
decay_rate = 0.95
tiny_value = 1e-06


def by_axis(x, axes):
    for axis in axes:
        x = lax.psum(x, axis)
    return x


def on_device(gradients, owners, block_param, left_stat, right_stat, moment, left_root, right_root):
    replicas = lax.axis_size(DP)
    capacity = left_stat.shape[0]
    blocks = gradients.shape[1]
    block_width = gradients.shape[3]
    device = lax.axis_index(DP)
    column = lax.axis_index(SHARD)
    owner_row = owners[0]
    counter = jnp.arange(blocks, dtype=jnp.int32)
    same_owner = owner_row[:, None] == owner_row[None, :]
    earlier = counter[None, :] < counter[:, None]
    places = owner_row * capacity + jnp.sum(jnp.where(same_owner & earlier, 1, 0), axis=1).astype(
        jnp.int32
    )
    slot_ids = jnp.arange(replicas * capacity, dtype=jnp.int32)
    matches = places[None, :] == slot_ids[:, None]
    source = jnp.min(jnp.where(matches, counter[None, :], blocks), axis=1)
    partials = gradients[0].astype(jnp.float32)
    row_share = lax.psum_scatter(partials, DP, scatter_dimension=1, tiled=True)
    share_padded = jnp.concatenate(
        [row_share, jnp.zeros((1,) + row_share.shape[1:], jnp.float32)], axis=0
    )
    outgoing = jnp.take(share_padded, source, axis=0).reshape(
        replicas, capacity, block_width // replicas, block_width
    )
    arrived = lax.all_to_all(outgoing, DP, split_axis=0, concat_axis=2, tiled=True)
    summed = arrived[0]
    left_gram = jnp.einsum("cij,ckj->cik", summed, summed, precision=lax.Precision.HIGHEST)
    right_gram = jnp.einsum("cji,cjk->cik", summed, summed, precision=lax.Precision.HIGHEST)
    new_left = decay_rate * left_stat + (1.0 - decay_rate) * left_gram[:, None]
    new_right = decay_rate * right_stat + (1.0 - decay_rate) * right_gram[:, None]
    new_moment = decay_rate * moment + (1.0 - decay_rate) * (summed * summed)[:, None]
    adam_step = summed / (jnp.sqrt(new_moment[:, 0]) + tiny_value)
    left_half = jnp.einsum(
        "cij,cjk->cik",
        left_root[:, 0],
        summed.astype(jnp.bfloat16),
        preferred_element_type=jnp.float32,
    ).astype(jnp.bfloat16)
    direction = jnp.einsum(
        "cij,cjk->cik", left_half, right_root[:, 0], preferred_element_type=jnp.float32
    )
    my_slots = lax.dynamic_slice_in_dim(matches, device * capacity, capacity, 0)
    local_params = lax.dynamic_slice_in_dim(block_param, column * blocks, blocks, 0)
    slot_param = jnp.sum(jnp.where(my_slots, local_params[None, :], 0), axis=1)
    is_live = jnp.any(my_slots, axis=1)
    param_ids = jnp.arange(NPARAM, dtype=jnp.int32)
    member = (slot_param[:, None] == param_ids[None, :]) & is_live[:, None]
    adam_squares = jnp.sum(adam_step * adam_step, axis=(1, 2))
    direction_squares = jnp.sum(direction * direction, axis=(1, 2))
    adam_local = jnp.sum(jnp.where(member, adam_squares[:, None], 0.0), axis=0)
    direction_local = jnp.sum(jnp.where(member, direction_squares[:, None], 0.0), axis=0)
    adam_norm, direction_norm = (by_axis(adam_local, DP_SHARD), by_axis(direction_local, DP_SHARD))
    graft_ratio = jnp.sqrt((adam_norm + tiny_value) / (direction_norm + tiny_value))
    slot_ratio = jnp.sum(jnp.where(member, graft_ratio[None, :], 0.0), axis=1)
    slot_update = (slot_ratio[:, None, None] * direction).astype(jnp.bfloat16)
    returned = lax.all_to_all(slot_update, DP, split_axis=1, concat_axis=0, tiled=True)
    pieces = jnp.take(returned, places, axis=0)
    update = lax.all_gather(pieces, DP, axis=1, tiled=True)
    return (new_left, new_right, new_moment, update)


def solution(mesh):
    finer = Mesh(
        mesh.devices.reshape(4, 2, 2, 4, 2), ("dp_0", "dp_1", "dp_2", "shard_0", "shard_1")
    )
    placed = (
        P(DP, SHARD, None, None),
        P(SHARD, None),
        P(),
        P(DP, SHARD, None, None),
        P(DP, SHARD, None, None),
        P(DP, SHARD, None, None),
        P(DP, SHARD, None, None),
        P(DP, SHARD, None, None),
    )
    return jax.shard_map(
        on_device,
        mesh=finer,
        in_specs=placed,
        out_specs=(
            P(DP, SHARD, None, None),
            P(DP, SHARD, None, None),
            P(DP, SHARD, None, None),
            P(SHARD, None, None),
        ),
        check_vma=False,
    )
```

profile of v0, /device:TPU:1, one launch (start us, length us, event | category | flops | bytes accessed | tf_op | source)
XLA Modules:
  0.0 309.6 jit_solution(17516869295652060086)
XLA Ops:
  7.2 0.0 copy-start
  7.2 0.0 reduce-scatter.2.cloned.1.call-start
  7.2 8.7 %bitcast_convert_fusion = f32[11,512,512]{2,1,0:T(8,128)} fusion(bf16[1,11,512,512]{3,2,1,0:T(8,128)(2,1)} %param.8), kind=kLoop, calls=%fused_computation.2 | loop fusion | flops 2883584 | bytes 17301504 | tf_op jit(solution)/shard_map/convert_element_type | solution.py:38
  15.9 0.0 copy-start.6
  15.9 0.0 reduce-scatter.2.cloned.1.call-update
  15.9 0.6 copy-done.6
  16.6 0.2 select_reduce_fusion.1
  16.7 0.1 select_reduce_fusion
  16.9 0.1 reduce_min.14
  17.0 130.2 %reduce-scatter.2.cloned.1.call-done = f32[11,32,512]{2,1,0:T(8,128)} async-done(((f32[11,512,512]{2,1,0:T(8,128)}), f32[11,32,512]{2,1,0:T(8,128)}) %reduce-scatter.2.cloned.1.call-update) | async-done | bytes 720912 | tf_op jit(solution)/shard_map/reduce_scatter | solution.py:39
  147.2 1.2 concatenate.3
  148.4 2.0 gather_fusion
  150.4 3.1 %broadcast_select_fusion = f32[16,2,32,512]{3,2,1,0:T(8,128)} fusion(f32[16,2,32,512]{3,2,1,0:T(8,128)} %bitcast.83, pred[16,2]{1,0:T(8,128)(4,1)S(1)} %compare_and_fusion), kind=kLoop, calls=%fused_computation.23 | loop fusion | flops 524288 | bytes 4194336 | tf_op jit(solution)/shard_map/jit(_take)/select_n | solution.py:43
  153.5 0.0 copy-start.5
  153.5 5.9 %all-to-all-start = ((f32[16,2,32,512]{3,2,1,0:T(8,128)}), f32[16,2,32,512]{3,2,1,0:T(8,128)S(1)}, u32[]{:S(2)}, u32[]{:S(2)}) async-start(f32[16,2,32,512]{3,2,1,0:T(8,128)} %broadcast_select_fusion), calls=%async_computation.1 | async-start | bytes 4194304 | tf_op jit(solution)/shard_map/all_to_all | solution.py:46
  159.3 0.0 copy-done.5
  159.3 0.1 dynamic_slice.7
  159.4 0.1 fusion.15
  159.5 0.1 select_reduce_fusion.5
  159.7 26.7 %all-to-all-done = f32[16,2,32,512]{3,2,1,0:T(8,128)S(1)} async-done(((f32[16,2,32,512]{3,2,1,0:T(8,128)}), f32[16,2,32,512]{3,2,1,0:T(8,128)S(1)}, u32[]{:S(2)}, u32[]{:S(2)}) %all-to-all-start) | async-done | bytes 2097184 | tf_op jit(solution)/shard_map/all_to_all | solution.py:46
  186.4 0.0 copy-start.2
  186.4 0.3 multiply_multiply_fusion
  186.6 1.1 copy-done.2
  187.7 0.2 copy.65
  187.9 0.0 copy-start.3
  188.0 2.0 copy.61
  189.9 0.3 copy-done.3
  190.2 2.8 sqrt_add_fusion
  192.9 0.0 copy-done
  193.0 4.0 %multiply_reduce_fusion = (f32[2]{0:T(128)S(1)}, f32[2,512,512]{2,1,0:T(8,128)}) fusion(bf16[2,1,512,512]{3,2,1,0:T(8,128)(2,1)S(1)} %copy-done, bf16[2,1,512,512]{3,2,1,0:T(8,128)(2,1)} %param.14, f32[2,512,512]{2,1,0:T(8,128)S(1)} %bitcast.79), kind=kOutput, calls=%fused_computation.14 | convolution fusion | flops 1075838976 | bytes 6291464 | tf_op jit(solution)/shard_map/cij,cjk->cik/dot_general | solution.py:60
  197.0 2.7 fusion.3
  199.6 0.1 select_reduce_fusion.4
  199.7 7.2 %all-reduce.2 = (f32[7]{0:T(128)S(1)}, f32[7]{0:T(128)S(1)}) all-reduce(f32[7]{0:T(128)S(1)} %get-tuple-element.25, f32[7]{0:T(128)S(1)} %get-tuple-element.24), channel_id=1, replica_groups=mesh['dp_0'=4,'dp_1'=2,'dp_2'=2,'shard_0'=4,'shard_1'=2] {'dp_0'}, use_global_device_ids=true, to_apply=%region_14.15 | all-reduce | flops 14 | bytes 112 | tf_op jit(solution)/shard_map/psum | solution.py:17
  206.9 3.8 %all-reduce.5 = (f32[7]{0:T(128)S(1)}, f32[7]{0:T(128)S(1)}) all-reduce(f32[7]{0:T(128)S(1)} %get-tuple-element.28, f32[7]{0:T(128)S(1)} %get-tuple-element.29), channel_id=1, replica_groups=mesh['dp_0'=4,'dp_1'=2,'dp_2'=2,'shard_0'=4,'shard_1'=2] {'dp_1'}, use_global_device_ids=true, to_apply=%region_15.16 | all-reduce | flops 14 | bytes 112 | tf_op jit(solution)/shard_map/psum | solution.py:17
  210.7 6.2 %all-reduce.4 = (f32[7]{0:T(128)S(1)}, f32[7]{0:T(128)S(1)}) all-reduce(f32[7]{0:T(128)S(1)} %get-tuple-element.34, f32[7]{0:T(128)S(1)} %get-tuple-element.35), channel_id=1, replica_groups=mesh['dp_0'=4,'dp_1'=2,'dp_2'=2,'shard_0'=4,'shard_1'=2] {'dp_2'}, use_global_device_ids=true, to_apply=%region_16.17 | all-reduce | flops 14 | bytes 112 | tf_op jit(solution)/shard_map/psum | solution.py:17
  216.9 8.7 %all-reduce.1 = (f32[7]{0:T(128)S(1)}, f32[7]{0:T(128)S(1)}) all-reduce(f32[7]{0:T(128)S(1)} %get-tuple-element.32, f32[7]{0:T(128)S(1)} %get-tuple-element.33), channel_id=1, replica_groups=mesh['dp_0'=4,'dp_1'=2,'dp_2'=2,'shard_0'=4,'shard_1'=2] {'shard_0'}, use_global_device_ids=true, to_apply=%region_17.18 | all-reduce | flops 14 | bytes 112 | tf_op jit(solution)/shard_map/psum | solution.py:17
  225.6 5.3 %all-reduce.3 = (f32[7]{0:T(128)S(1)}, f32[7]{0:T(128)S(1)}) all-reduce(f32[7]{0:T(128)S(1)} %get-tuple-element.26, f32[7]{0:T(128)S(1)} %get-tuple-element.27), channel_id=1, replica_groups=mesh['dp_0'=4,'dp_1'=2,'dp_2'=2,'shard_0'=4,'shard_1'=2] {'shard_1'}, use_global_device_ids=true, to_apply=%region_18.19 | all-reduce | flops 14 | bytes 112 | tf_op jit(solution)/shard_map/psum | solution.py:17
  230.9 0.2 select_reduce_fusion.2
  231.1 1.9 multiply_convert_fusion
  233.0 2.0 copy.69
  235.0 7.0 %all-to-all-start.1 = ((bf16[2,512,512]{2,0,1:T(2,128)(2,1)}), bf16[2,512,512]{2,0,1:T(2,128)(2,1)S(1)}, u32[]{:S(2)}, u32[]{:S(2)}) async-start(bf16[2,512,512]{2,0,1:T(2,128)(2,1)} %copy.69), calls=%async_computation.2 | async-start | bytes 2097152 | tf_op jit(solution)/shard_map/all_to_all | solution.py:77
  242.0 0.2 all-gather.2.cloned.1.call-start
  242.2 15.5 %all-to-all-done.1 = bf16[2,512,512]{2,0,1:T(2,128)(2,1)S(1)} async-done(((bf16[2,512,512]{2,0,1:T(2,128)(2,1)}), bf16[2,512,512]{2,0,1:T(2,128)(2,1)S(1)}, u32[]{:S(2)}, u32[]{:S(2)}) %all-to-all-start.1) | async-done | bytes 1048608 | tf_op jit(solution)/shard_map/all_to_all | solution.py:77
  257.7 0.2 copy.70
  257.9 0.1 copy.71
  258.0 0.6 gather_fusion.1
  258.6 0.8 broadcast_select_fusion.1
  259.4 0.0 all-gather.2.cloned.1.call-update
  259.4 0.0 copy-start.4
  259.4 6.1 %fusion = f32[2,1,512,512]{3,2,1,0:T(8,128)} fusion(f32[2,1,512,512]{3,2,1,0:T(8,128)} %param.12, f32[2,512,512]{2,1,0:T(8,128)S(1)} %bitcast.80), kind=kOutput, calls=%fused_computation.6 | convolution fusion | flops 3222798336 | bytes 6291456 | tf_op jit(solution)/shard_map/cji,cjk->cik/dot_general | solution.py:49
  265.6 0.0 copy-done.4
  265.6 5.0 %fusion.1 = f32[2,1,512,512]{3,2,1,0:T(8,128)} fusion(f32[2,1,512,512]{3,2,1,0:T(8,128)S(1)} %copy-done.4, f32[2,512,512]{2,1,0:T(8,128)S(1)} %bitcast.81), kind=kOutput, calls=%fused_computation.9 | convolution fusion | flops 3222798336 | bytes 6291456 | tf_op jit(solution)/shard_map/cij,ckj->cik/dot_general | solution.py:48
  270.6 26.5 %all-gather.2.cloned.1.call-done = bf16[11,512,512]{2,1,0:T(8,128)(2,1)} async-done(((bf16[11,32,512]{2,1,0:T(8,128)(2,1)}), bf16[11,512,512]{2,1,0:T(8,128)(2,1)}) %all-gather.2.cloned.1.call-update) | async-done | bytes 5767184 | tf_op jit(solution)/shard_map/all_gather | solution.py:79
  297.1 0.0 copy-start.1
  297.1 5.6 %copy.85 = bf16[11,512,512]{2,1,0:T(8,128)(2,1)} copy(bf16[11,512,512]{2,1,0:T(8,128)(2,1)} %all-gather.2.cloned.1.call-done) | data formatting | bytes 11534336
  302.7 0.0 copy-done.1
  (9 shorter events, 0.1 us)
Async XLA Ops:
  7.2 185.8 %copy-start = (bf16[2,1,512,512]{3,2,1,0:T(8,128)(2,1)S(1)}, bf16[2,1,512,512]{3,2,1,0:T(8,128)(2,1)}, u32[]{:S(2)}) copy-start(bf16[2,1,512,512]{3,2,1,0:T(8,128)(2,1)} %param.15) | copy-start | bytes 3145732
  7.2 140.0 %reduce-scatter.2.cloned.1.call-start = ((), (), s32[]{:S(2)}) async-start(), calls=%async_computation.3 | async-start | bytes 12255232 | tf_op jit(solution)/shard_map/reduce_scatter | solution.py:39
  15.9 0.7 copy-start.6
  153.5 5.9 %copy-start.5 = (s32[88]{0:T(128)S(1)}, s32[88]{0:T(128)}, u32[]{:S(2)}) copy-start(s32[88]{0:T(128)} %param.10) | copy-start | bytes 1060
  153.5 32.9 %all-to-all-start = ((f32[16,2,32,512]{3,2,1,0:T(8,128)}), f32[16,2,32,512]{3,2,1,0:T(8,128)S(1)}, u32[]{:S(2)}, u32[]{:S(2)}) async-start(f32[16,2,32,512]{3,2,1,0:T(8,128)} %broadcast_select_fusion), calls=%async_computation.1 | async-start | bytes 4194304 | tf_op jit(solution)/shard_map/all_to_all | solution.py:46
  186.4 1.3 copy-start.2
  187.9 2.2 copy-start.3
  235.0 22.7 %all-to-all-start.1 = ((bf16[2,512,512]{2,0,1:T(2,128)(2,1)}), bf16[2,512,512]{2,0,1:T(2,128)(2,1)S(1)}, u32[]{:S(2)}, u32[]{:S(2)}) async-start(bf16[2,512,512]{2,0,1:T(2,128)(2,1)} %copy.69), calls=%async_computation.2 | async-start | bytes 2097152 | tf_op jit(solution)/shard_map/all_to_all | solution.py:77
  242.0 55.1 %all-gather.2.cloned.1.call-start = ((), (), s32[]{:S(2)}) async-start(), calls=%async_computation.4 | async-start | bytes 6127616 | tf_op jit(solution)/shard_map/all_gather | solution.py:79
  259.4 6.2 %copy-start.4 = (f32[2,1,512,512]{3,2,1,0:T(8,128)S(1)}, f32[2,1,512,512]{3,2,1,0:T(8,128)}, u32[]{:S(2)}) copy-start(f32[2,1,512,512]{3,2,1,0:T(8,128)} %param.11) | copy-start | bytes 6291460
  297.1 5.6 %copy-start.1 = (bf16[2,1,512,512]{3,2,1,0:T(8,128)(2,1)S(1)}, bf16[2,1,512,512]{3,2,1,0:T(8,128)(2,1)}, u32[]{:S(2)}) copy-start(bf16[2,1,512,512]{3,2,1,0:T(8,128)(2,1)} %param.15) | copy-start | bytes 3145732
Sparse Core Ops, SparseCore 0:
  16.0 131.0 reduce-scatter.1
  259.6 37.5 all-gather.1
where the time goes:
time: 310 us
  waiting for transfers between devices  199 us (64%)
  blocking collectives  31.1 us (10%)
  other arithmetic  21.1 us (7%)
  local copies, waits for them, and re-layouts  16 us (5%)
  matrix products  15.1 us (5%)
  between operations  14.2 us (5%)
  starting transfers between devices  13.1 us (4%)
    reduce_scatter x1, waiting for transfers between devices, on_device(): row_share = lax.psum_scatter(partials, DP, scatter_dimension=1, tiled=True)  130 us
    psum x5, blocking collectives, by_axis(): x = lax.psum(x, axis)  31.1 us
    all_to_all x1, waiting for transfers between devices, on_device(): lax.all_to_all(outgoing, DP, split_axis=0, concat_axis=2, tiled=True)  26.7 us
    all_gather x1, waiting for transfers between devices, on_device(): update = lax.all_gather(pieces, DP, axis=1, tiled=True)  26.5 us
    all_to_all x1, waiting for transfers between devices, on_device(): lax.all_to_all(slot_update, DP, split_axis=1, concat_axis=0, tiled=True)  15.5 us
    convert_element_type x1, other arithmetic, on_device(): partials = gradients[0].astype(jnp.float32)  8.67 us
    unnamed x15, local copies, waits for them, and re-layouts  7.59 us
    all_to_all x1, starting transfers between devices, on_device(): lax.all_to_all(slot_update, DP, split_axis=1, concat_axis=0, tiled=True)  6.96 us
  transfers between devices with their start and end apart: 4, of which 4 were waited for; matrix products, arithmetic and copies ran while one was open for 4% of the time, Pallas kernels for 0%

commit v1 on v0

--- a/solution.py
+++ b/solution.py
@@ -76,7 +76,7 @@
     slot_update = (slot_ratio[:, None, None] * direction).astype(jnp.bfloat16)
     returned = lax.all_to_all(slot_update, DP, split_axis=1, concat_axis=0, tiled=True)
     pieces = jnp.take(returned, places, axis=0)
-    update = lax.all_gather(pieces, DP, axis=1, tiled=True)
+    update = jnp.concatenate(lax.all_gather(pieces, DP), axis=1)
     return (new_left, new_right, new_moment, update)
 
 

time: 310 us -> 311 us (level)
    all_gather x0 -> x1, local copies, waits for them, and re-layouts: none -> 6.24 us  [on_device(): update = jnp.concatenate(lax.all_gather(pieces, DP), axis=1)]
    unnamed x15 -> x14, local copies, waits for them, and re-layouts: 7.59 us -> 1.97 us
where the time goes in v1:
time: 311 us; the launch traced here: 310 us
  waiting for transfers between devices  199 us (64%)
  blocking collectives  31.1 us (10%)
  other arithmetic  21.1 us (7%)
  local copies, waits for them, and re-layouts  16.6 us (5%)
  matrix products  15.1 us (5%)
  between operations  14.2 us (5%)
  starting transfers between devices  13.1 us (4%)
    reduce_scatter x1, waiting for transfers between devices, on_device(): row_share = lax.psum_scatter(partials, DP, scatter_dimension=1, tiled=True)  130 us
    psum x5, blocking collectives, by_axis(): x = lax.psum(x, axis)  31.1 us
    all_to_all x1, waiting for transfers between devices, on_device(): lax.all_to_all(outgoing, DP, split_axis=0, concat_axis=2, tiled=True)  26.7 us
    all_gather x1, waiting for transfers between devices, on_device(): update = jnp.concatenate(lax.all_gather(pieces, DP), axis=1)  26.5 us
    all_to_all x1, waiting for transfers between devices, on_device(): lax.all_to_all(slot_update, DP, split_axis=1, concat_axis=0, tiled=True)  15.5 us
    convert_element_type x1, other arithmetic, on_device(): partials = gradients[0].astype(jnp.float32)  8.67 us
    all_to_all x1, starting transfers between devices, on_device(): lax.all_to_all(slot_update, DP, split_axis=1, concat_axis=0, tiled=True)  6.96 us
    all_gather x1, local copies, waits for them, and re-layouts, on_device(): update = jnp.concatenate(lax.all_gather(pieces, DP), axis=1)  6.24 us
  transfers between devices with their start and end apart: 4, of which 4 were waited for; matrix products, arithmetic and copies ran while one was open for 4% of the time, Pallas kernels for 0%

profile of v1, /device:TPU:1, one launch (start us, length us, event | category | flops | bytes accessed | tf_op | source)
XLA Modules:
  0.0 310.2 jit_solution(6380251107127345327)
XLA Ops:
  7.2 0.0 copy-start
  7.2 0.0 reduce-scatter.2.cloned.1.call-start
  7.2 8.7 %bitcast_convert_fusion = f32[11,512,512]{2,1,0:T(8,128)} fusion(bf16[1,11,512,512]{3,2,1,0:T(8,128)(2,1)} %param.8), kind=kLoop, calls=%fused_computation.2 | loop fusion | flops 2883584 | bytes 17301504 | tf_op jit(solution)/shard_map/convert_element_type | solution.py:38
  15.9 0.0 copy-start.6
  15.9 0.0 reduce-scatter.2.cloned.1.call-update
  15.9 0.6 copy-done.6
  16.6 0.2 select_reduce_fusion.1
  16.7 0.1 select_reduce_fusion
  16.9 0.1 reduce_min.14
  17.0 130.2 %reduce-scatter.2.cloned.1.call-done = f32[11,32,512]{2,1,0:T(8,128)} async-done(((f32[11,512,512]{2,1,0:T(8,128)}), f32[11,32,512]{2,1,0:T(8,128)}) %reduce-scatter.2.cloned.1.call-update) | async-done | bytes 720912 | tf_op jit(solution)/shard_map/reduce_scatter | solution.py:39
  147.2 1.2 concatenate.3
  148.4 2.0 gather_fusion
  150.4 3.1 %broadcast_select_fusion = f32[16,2,32,512]{3,2,1,0:T(8,128)} fusion(f32[16,2,32,512]{3,2,1,0:T(8,128)} %bitcast.88, pred[16,2]{1,0:T(8,128)(4,1)S(1)} %compare_and_fusion), kind=kLoop, calls=%fused_computation.23 | loop fusion | flops 524288 | bytes 4194336 | tf_op jit(solution)/shard_map/jit(_take)/select_n | solution.py:43
  153.5 0.0 copy-start.5
  153.5 5.9 %all-to-all-start = ((f32[16,2,32,512]{3,2,1,0:T(8,128)}), f32[16,2,32,512]{3,2,1,0:T(8,128)S(1)}, u32[]{:S(2)}, u32[]{:S(2)}) async-start(f32[16,2,32,512]{3,2,1,0:T(8,128)} %broadcast_select_fusion), calls=%async_computation.1 | async-start | bytes 4194304 | tf_op jit(solution)/shard_map/all_to_all | solution.py:46
  159.3 0.0 copy-done.5
  159.3 0.1 dynamic_slice.7
  159.4 0.1 fusion.15
  159.5 0.1 select_reduce_fusion.5
  159.7 26.7 %all-to-all-done = f32[16,2,32,512]{3,2,1,0:T(8,128)S(1)} async-done(((f32[16,2,32,512]{3,2,1,0:T(8,128)}), f32[16,2,32,512]{3,2,1,0:T(8,128)S(1)}, u32[]{:S(2)}, u32[]{:S(2)}) %all-to-all-start) | async-done | bytes 2097184 | tf_op jit(solution)/shard_map/all_to_all | solution.py:46
  186.4 0.0 copy-start.2
  186.4 0.3 multiply_multiply_fusion
  186.6 1.1 copy-done.2
  187.7 0.2 copy.80
  187.9 0.0 copy-start.3
  188.0 2.0 copy.76
  189.9 0.3 copy-done.3
  190.2 2.8 sqrt_add_fusion
  192.9 0.0 copy-done
  193.0 4.0 %multiply_reduce_fusion = (f32[2]{0:T(128)S(1)}, f32[2,512,512]{2,1,0:T(8,128)}) fusion(bf16[2,1,512,512]{3,2,1,0:T(8,128)(2,1)S(1)} %copy-done, bf16[2,1,512,512]{3,2,1,0:T(8,128)(2,1)} %param.14, f32[2,512,512]{2,1,0:T(8,128)S(1)} %bitcast.84), kind=kOutput, calls=%fused_computation.14 | convolution fusion | flops 1075838976 | bytes 6291464 | tf_op jit(solution)/shard_map/cij,cjk->cik/dot_general | solution.py:60
  197.0 2.7 fusion.3
  199.6 0.1 select_reduce_fusion.4
  199.7 7.2 %all-reduce.2 = (f32[7]{0:T(128)S(1)}, f32[7]{0:T(128)S(1)}) all-reduce(f32[7]{0:T(128)S(1)} %get-tuple-element.29, f32[7]{0:T(128)S(1)} %get-tuple-element.28), channel_id=1, replica_groups=mesh['dp_0'=4,'dp_1'=2,'dp_2'=2,'shard_0'=4,'shard_1'=2] {'dp_0'}, use_global_device_ids=true, to_apply=%region_14.15 | all-reduce | flops 14 | bytes 112 | tf_op jit(solution)/shard_map/psum | solution.py:17
  206.9 3.8 %all-reduce.5 = (f32[7]{0:T(128)S(1)}, f32[7]{0:T(128)S(1)}) all-reduce(f32[7]{0:T(128)S(1)} %get-tuple-element.32, f32[7]{0:T(128)S(1)} %get-tuple-element.33), channel_id=1, replica_groups=mesh['dp_0'=4,'dp_1'=2,'dp_2'=2,'shard_0'=4,'shard_1'=2] {'dp_1'}, use_global_device_ids=true, to_apply=%region_15.16 | all-reduce | flops 14 | bytes 112 | tf_op jit(solution)/shard_map/psum | solution.py:17
  210.7 6.2 %all-reduce.4 = (f32[7]{0:T(128)S(1)}, f32[7]{0:T(128)S(1)}) all-reduce(f32[7]{0:T(128)S(1)} %get-tuple-element.38, f32[7]{0:T(128)S(1)} %get-tuple-element.39), channel_id=1, replica_groups=mesh['dp_0'=4,'dp_1'=2,'dp_2'=2,'shard_0'=4,'shard_1'=2] {'dp_2'}, use_global_device_ids=true, to_apply=%region_16.17 | all-reduce | flops 14 | bytes 112 | tf_op jit(solution)/shard_map/psum | solution.py:17
  216.9 8.7 %all-reduce.1 = (f32[7]{0:T(128)S(1)}, f32[7]{0:T(128)S(1)}) all-reduce(f32[7]{0:T(128)S(1)} %get-tuple-element.36, f32[7]{0:T(128)S(1)} %get-tuple-element.37), channel_id=1, replica_groups=mesh['dp_0'=4,'dp_1'=2,'dp_2'=2,'shard_0'=4,'shard_1'=2] {'shard_0'}, use_global_device_ids=true, to_apply=%region_17.18 | all-reduce | flops 14 | bytes 112 | tf_op jit(solution)/shard_map/psum | solution.py:17
  225.6 5.3 %all-reduce.3 = (f32[7]{0:T(128)S(1)}, f32[7]{0:T(128)S(1)}) all-reduce(f32[7]{0:T(128)S(1)} %get-tuple-element.30, f32[7]{0:T(128)S(1)} %get-tuple-element.31), channel_id=1, replica_groups=mesh['dp_0'=4,'dp_1'=2,'dp_2'=2,'shard_0'=4,'shard_1'=2] {'shard_1'}, use_global_device_ids=true, to_apply=%region_18.19 | all-reduce | flops 14 | bytes 112 | tf_op jit(solution)/shard_map/psum | solution.py:17
  230.9 0.2 select_reduce_fusion.2
  231.1 1.9 multiply_convert_fusion
  233.0 2.0 copy.84
  235.0 7.0 %all-to-all-start.1 = ((bf16[2,512,512]{2,0,1:T(2,128)(2,1)}), bf16[2,512,512]{2,0,1:T(2,128)(2,1)S(1)}, u32[]{:S(2)}, u32[]{:S(2)}) async-start(bf16[2,512,512]{2,0,1:T(2,128)(2,1)} %copy.84), calls=%async_computation.2 | async-start | bytes 2097152 | tf_op jit(solution)/shard_map/all_to_all | solution.py:77
  242.0 0.2 all-gather.2.cloned.1.call-start
  242.2 15.5 %all-to-all-done.1 = bf16[2,512,512]{2,0,1:T(2,128)(2,1)S(1)} async-done(((bf16[2,512,512]{2,0,1:T(2,128)(2,1)}), bf16[2,512,512]{2,0,1:T(2,128)(2,1)S(1)}, u32[]{:S(2)}, u32[]{:S(2)}) %all-to-all-start.1) | async-done | bytes 1048608 | tf_op jit(solution)/shard_map/all_to_all | solution.py:77
  257.7 0.2 copy.85
  257.9 0.1 copy.86
  258.0 0.6 gather_fusion.1
  258.6 0.8 bitcast_select_fusion
  259.4 0.0 all-gather.2.cloned.1.call-update
  259.4 0.0 copy-start.4
  259.4 6.1 %fusion = f32[2,1,512,512]{3,2,1,0:T(8,128)} fusion(f32[2,1,512,512]{3,2,1,0:T(8,128)} %param.12, f32[2,512,512]{2,1,0:T(8,128)S(1)} %bitcast.85), kind=kOutput, calls=%fused_computation.6 | convolution fusion | flops 3222798336 | bytes 6291456 | tf_op jit(solution)/shard_map/cji,cjk->cik/dot_general | solution.py:49
  265.6 0.0 copy-done.4
  265.6 5.0 %fusion.1 = f32[2,1,512,512]{3,2,1,0:T(8,128)} fusion(f32[2,1,512,512]{3,2,1,0:T(8,128)S(1)} %copy-done.4, f32[2,512,512]{2,1,0:T(8,128)S(1)} %bitcast.86), kind=kOutput, calls=%fused_computation.9 | convolution fusion | flops 3222798336 | bytes 6291456 | tf_op jit(solution)/shard_map/cij,ckj->cik/dot_general | solution.py:48
  270.6 26.5 %all-gather.2.cloned.1.call-done = bf16[16,11,32,512]{3,2,1,0:T(8,128)(2,1)} async-done(((bf16[1,11,32,512]{3,2,1,0:T(8,128)(2,1)}), bf16[16,11,32,512]{3,2,1,0:T(8,128)(2,1)}) %all-gather.2.cloned.1.call-update) | async-done | bytes 5767184 | tf_op jit(solution)/shard_map/all_gather | solution.py:79
  297.1 0.0 copy-start.1
  297.1 6.2 %copy.87 = bf16[16,11,32,512]{3,2,0,1:T(8,128)(2,1)} copy(bf16[16,11,32,512]{3,2,1,0:T(8,128)(2,1)} %all-gather.2.cloned.1.call-done) | data formatting | bytes 11534336 | tf_op jit(solution)/shard_map/all_gather | solution.py:79
  303.4 0.0 copy-done.1
  (9 shorter events, 0.1 us)
Async XLA Ops:
  7.2 185.8 %copy-start = (bf16[2,1,512,512]{3,2,1,0:T(8,128)(2,1)S(1)}, bf16[2,1,512,512]{3,2,1,0:T(8,128)(2,1)}, u32[]{:S(2)}) copy-start(bf16[2,1,512,512]{3,2,1,0:T(8,128)(2,1)} %param.15) | copy-start | bytes 3145732
  7.2 140.0 %reduce-scatter.2.cloned.1.call-start = ((), (), s32[]{:S(2)}) async-start(), calls=%async_computation.3 | async-start | bytes 12255232 | tf_op jit(solution)/shard_map/reduce_scatter | solution.py:39
  15.9 0.7 copy-start.6
  153.5 5.9 %copy-start.5 = (s32[88]{0:T(128)S(1)}, s32[88]{0:T(128)}, u32[]{:S(2)}) copy-start(s32[88]{0:T(128)} %param.10) | copy-start | bytes 1060
  153.5 32.9 %all-to-all-start = ((f32[16,2,32,512]{3,2,1,0:T(8,128)}), f32[16,2,32,512]{3,2,1,0:T(8,128)S(1)}, u32[]{:S(2)}, u32[]{:S(2)}) async-start(f32[16,2,32,512]{3,2,1,0:T(8,128)} %broadcast_select_fusion), calls=%async_computation.1 | async-start | bytes 4194304 | tf_op jit(solution)/shard_map/all_to_all | solution.py:46
  186.4 1.3 copy-start.2
  187.9 2.2 copy-start.3
  235.0 22.7 %all-to-all-start.1 = ((bf16[2,512,512]{2,0,1:T(2,128)(2,1)}), bf16[2,512,512]{2,0,1:T(2,128)(2,1)S(1)}, u32[]{:S(2)}, u32[]{:S(2)}) async-start(bf16[2,512,512]{2,0,1:T(2,128)(2,1)} %copy.84), calls=%async_computation.2 | async-start | bytes 2097152 | tf_op jit(solution)/shard_map/all_to_all | solution.py:77
  242.0 55.1 %all-gather.2.cloned.1.call-start = ((), (), s32[]{:S(2)}) async-start(), calls=%async_computation.4 | async-start | bytes 6127616 | tf_op jit(solution)/shard_map/all_gather | solution.py:79
  259.4 6.2 %copy-start.4 = (f32[2,1,512,512]{3,2,1,0:T(8,128)S(1)}, f32[2,1,512,512]{3,2,1,0:T(8,128)}, u32[]{:S(2)}) copy-start(f32[2,1,512,512]{3,2,1,0:T(8,128)} %param.11) | copy-start | bytes 6291460
  297.1 6.2 %copy-start.1 = (bf16[2,1,512,512]{3,2,1,0:T(8,128)(2,1)S(1)}, bf16[2,1,512,512]{3,2,1,0:T(8,128)(2,1)}, u32[]{:S(2)}) copy-start(bf16[2,1,512,512]{3,2,1,0:T(8,128)(2,1)} %param.15) | copy-start | bytes 3145732
Sparse Core Ops, SparseCore 0:
  16.0 131.0 reduce-scatter.1
  259.6 37.5 all-gather.1
